TPU v7x, 1024 devices: a whole 4x4x32 slice. The times are simulated.
1024 devices in a mesh: dp: 4 (over y), fsdp: 256 (over z, x, core).
Axes of the slice: x: 4, y: 4, z: 32, core: 2. Of those that a mesh axis runs over, the one named last changes fastest.
Arguments:
- grad: bfloat16 [4, 8192, 14336], P('dp', 'fsdp'), may hold values from -120 to 120
- error: bfloat16 [4, 8192, 14336], P('dp', 'fsdp'), may hold values from -3 to 3
- q_init: float32 [14336, 32], replicated, may hold values from -6 to 6
Outputs:
- update: float32 [8192, 14336], P('fsdp')
- new_error: bfloat16 [4, 8192, 14336], P('dp', 'fsdp')
All inputs are finite; a program needn't handle non-finite values.
Results may differ from a plain program's by a relative error of at most 0.001.
Values sent between devices are 32-bit elements; how exact they have to be, the bound alone decides.
A program may use at most 64 MiB of HBM per device.

v0:
```python
import jax
import jax.numpy as jnp
from jax import lax
from jax.sharding import Mesh
from jax.sharding import PartitionSpec as P

FSDP = ("fsdp_0", "fsdp_1", "fsdp_2")


def copy_for_each(array, axis):
    devices = lax.axis_size(axis)
    return lax.all_to_all(
        jnp.broadcast_to(array[None], (devices, *array.shape)), axis, 0, 0, tiled=True
    )


def taken_together(array, axis):
    everything = copy_for_each(array, axis)
    return jnp.sum(everything, axis=0)


def over_axes(array, axes):
    for axis in axes:
        array = lax.psum(array, axis)
    return array


def own_block(parts, axes, turns):
    shape = [lax.axis_size(a) for a in axes]
    parts = parts.reshape(*shape, *parts.shape[1:])
    parts = parts.transpose(*turns, *range(len(axes), parts.ndim))
    parts = parts.reshape(-1, *parts.shape[len(axes) :])
    for k in turns:
        parts = lax.psum_scatter(parts, axes[k], scatter_dimension=0, tiled=True)
    return parts[0]


def split_up(array, dim, devices):
    shape = array.shape
    parts = array.reshape(*shape[:dim], devices, shape[dim] // devices, *shape[dim + 1 :])
    return jnp.moveaxis(parts, dim, 0)


def summed_rows(array, axes, turns, dim):
    devices = lax.axis_size(axes)
    return own_block(split_up(array, dim, devices), axes, turns)


def in_order(parts, dim):
    shape = list(parts.shape[1:])
    shape[dim] *= parts.shape[0]
    return jnp.moveaxis(parts, 0, dim).reshape(shape)


def gather_in_order(array, axes, turns):
    parts = array
    for k in turns:
        parts = lax.all_gather(parts, axes[k])
    done = turns[::-1]
    back = [done.index(k) for k in range(len(axes))]
    parts = parts.transpose(*back, *range(len(axes), parts.ndim))
    return parts.reshape(-1, *array.shape)


def gathered_by_axis(array, axes, turns, dim):
    return in_order(gather_in_order(array, axes, turns), dim)


def body(grad, error, q_init):
    merged = grad[0].astype(jnp.float32) + error[0].astype(jnp.float32)
    p_local = jnp.dot(merged, q_init, precision=lax.Precision.HIGHEST)
    p_sum = taken_together(p_local, "dp")
    gram_local = lax.dot_general(
        p_sum, p_sum, (((0,), (0,)), ((), ())), precision=lax.Precision.HIGHEST
    )
    gram = over_axes(gram_local, FSDP)
    lower = jnp.linalg.cholesky(gram)
    p_hat = jax.scipy.linalg.solve_triangular(lower, p_sum.T, lower=True).T
    q_local = lax.dot_general(
        merged, p_hat, (((0,), (0,)), ((), ())), precision=lax.Precision.HIGHEST
    )
    inverse = 1.0 / lax.axis_size("dp")
    share = summed_rows(q_local, FSDP, (2, 0, 1), 0)
    share = taken_together(share, "dp") * inverse
    update = lax.dot_general(
        p_hat,
        gathered_by_axis(share, FSDP, (0, 1, 2), 0),
        (((1,), (1,)), ((), ())),
        precision=lax.Precision.HIGHEST,
    )
    new_error = (merged - update).astype(jnp.bfloat16)[None]
    return (update, new_error)


def solution(mesh):
    split = Mesh(
        mesh.devices.reshape(mesh.shape["dp"], 32, 4, 2), ("dp", "fsdp_0", "fsdp_1", "fsdp_2")
    )
    placed = (P("dp", FSDP, None), P("dp", FSDP, None), P())
    return jax.shard_map(
        body,
        mesh=split,
        in_specs=placed,
        out_specs=(P(FSDP, None), P("dp", FSDP, None)),
        check_vma=False,
    )
```

profile of v0, /device:TPU:1, one launch (start us, length us, event | category | flops | bytes accessed | tf_op | source)
XLA Modules:
  0.0 541.3 jit_solution(17361227141333718731)
XLA Ops:
  7.2 0.0 copy-start
  7.2 0.0 copy-start.1
  7.2 1.5 copy-done
  8.7 3.2 fusion.5
  11.9 0.7 reshape.39
  12.6 5.0 all-to-all-start
  17.6 0.0 reduce-scatter.4.cloned.1.call-start
  17.6 0.0 copy-done.1
  17.6 2.6 fusion.8
  20.2 10.2 %dot_general.19 = f32[32,4,2,56,32]{3,2,1,0,4:T(2,128)} reshape(f32[14336,32]{0,1:T(8,128)} %fusion.8) | data formatting | bytes 3670016 | tf_op jit(solution)/shard_map/dot_general | solution.py:79
  30.4 0.0 all-to-all-done
  30.4 0.5 broadcast.63
  30.9 0.7 reduce.6
  31.6 0.1 reshape.40
  31.7 0.2 fusion.15
  31.9 93.0 %psum.21 = f32[32,32]{0,1:T(8,128)S(1)} all-reduce(f32[32,32]{0,1:T(8,128)S(1)} %fusion.15), channel_id=1, replica_groups=mesh['dp'=4,'fsdp_0'=32,'fsdp_1'=4,'fsdp_2'=2] {'fsdp_0'}, use_global_device_ids=true, to_apply=%region_1.0 | all-reduce | flops 1024 | bytes 8192 | tf_op jit(solution)/shard_map/psum | solution.py:24
  125.0 13.1 %psum.22 = f32[32,32]{0,1:T(8,128)S(1)} all-reduce(f32[32,32]{0,1:T(8,128)S(1)} %psum.21), channel_id=1, replica_groups=mesh['dp'=4,'fsdp_0'=32,'fsdp_1'=4,'fsdp_2'=2] {'fsdp_1'}, use_global_device_ids=true, to_apply=%region_2.0 | all-reduce | flops 1024 | bytes 8192 | tf_op jit(solution)/shard_map/psum | solution.py:24
  138.1 35.5 %psum.23 = f32[32,32]{0,1:T(8,128)S(1)} all-reduce(f32[32,32]{0,1:T(8,128)S(1)} %psum.22), channel_id=1, replica_groups=mesh['dp'=4,'fsdp_0'=32,'fsdp_1'=4,'fsdp_2'=2] {'fsdp_2'}, use_global_device_ids=true, to_apply=%region_3.0 | all-reduce | flops 1024 | bytes 8192 | tf_op jit(solution)/shard_map/psum | solution.py:24
  173.6 0.1 copy.25
  173.7 2.9 cholesky.16
  176.7 0.6 compare_reduce_fusion
  177.3 0.7 fusion.10
  178.0 2.4 custom-call.7
  180.4 0.2 fusion.12
  180.6 8.4 %fusion.2 = f32[2,32,4,56,32]{3,4,0,2,1:T(8,128)S(1)} fusion(f32[32,4,2,56,32]{3,2,1,0,4:T(2,128)} %dot_general.19, f32[32,32]{1,0:T(8,128)S(1)} %fusion.12), kind=kOutput, calls=%fused_computation.2 | convolution fusion | flops 176160768 | bytes 3674112 | tf_op jit(solution)/shard_map/dot_general | solution.py:79
  189.0 2.6 copy.27
  191.6 0.0 reduce-scatter.4.cloned.1.call-update
  191.6 0.0 reduce-scatter.6.cloned.1.call-start
  191.7 24.7 %reduce-scatter.4.cloned.1.call-done = f32[128,56,32]{1,2,0:T(8,128)} async-done(((f32[256,56,32]{1,2,0:T(8,128)}), f32[128,56,32]{1,2,0:T(8,128)}) %reduce-scatter.4.cloned.1.call-update) | async-done | bytes 917520 | tf_op jit(solution)/shard_map/reduce_scatter | solution.py:34
  216.4 0.0 reduce-scatter.6.cloned.1.call-update
  216.4 0.0 reduce-scatter.8.cloned.1.call-start
  216.5 119.7 %reduce-scatter.6.cloned.1.call-done = f32[4,56,32]{1,2,0:T(8,128)} async-done(((f32[128,56,32]{1,2,0:T(8,128)}), f32[4,56,32]{1,2,0:T(8,128)}) %reduce-scatter.6.cloned.1.call-update) | async-done | bytes 28688 | tf_op jit(solution)/shard_map/reduce_scatter | solution.py:34
  336.2 0.0 reduce-scatter.8.cloned.1.call-update
  336.2 0.0 all-gather.6.cloned.1.call-start
  336.3 56.4 %reduce-scatter.8.cloned.1.call-done = f32[1,56,32]{1,2,0:T(8,128)} async-done(((f32[4,56,32]{1,2,0:T(8,128)}), f32[1,56,32]{1,2,0:T(8,128)}) %reduce-scatter.8.cloned.1.call-update) | async-done | bytes 7184 | tf_op jit(solution)/shard_map/reduce_scatter | solution.py:34
  392.7 0.7 broadcast_bitcast_fusion
  393.4 0.1 reshape.41
  393.5 8.0 %all_to_all.10 = f32[4,1,1792]{2,1,0:T(1,128)S(1)} all-to-all(f32[4,1,1792]{2,1,0:T(1,128)S(1)} %reshape.41), channel_id=1, replica_groups=mesh['dp'=4,'fsdp_0'=32,'fsdp_1'=4,'fsdp_2'=2] {'dp'}, dimensions={0} | all-to-all | bytes 57344 | tf_op jit(solution)/shard_map/all_to_all | solution.py:12
  401.5 0.7 reduce.7
  402.2 0.1 reshape.42
  402.3 46.7 %all-gather.3 = f32[32,56,32]{1,2,0:T(8,128)S(1)} all-gather(f32[1,56,32]{1,2,0:T(8,128)S(1)} %multiply_bitcast_fusion), channel_id=2, replica_groups=mesh['dp'=4,'fsdp_0'=32,'fsdp_1'=4,'fsdp_2'=2] {'fsdp_0'}, dimensions={0}, use_global_device_ids=true | all-gather | bytes 236544 | tf_op jit(solution)/shard_map/all_gather | solution.py:58
  449.1 14.0 %all-gather.1 = f32[128,56,32]{1,2,0:T(8,128)} all-gather(f32[32,56,32]{1,2,0:T(8,128)S(1)} %all-gather.3), channel_id=3, replica_groups=mesh['dp'=4,'fsdp_0'=32,'fsdp_1'=4,'fsdp_2'=2] {'fsdp_1'}, dimensions={0}, use_global_device_ids=true | all-gather | bytes 1146880 | tf_op jit(solution)/shard_map/all_gather | solution.py:58
  463.1 0.0 all-gather.6.cloned.1.call-update
  463.1 50.2 %all-gather.6.cloned.1.call-done = f32[8,32,56,32]{2,3,1,0:T(8,128)} async-done(((f32[4,32,56,32]{2,3,1,0:T(8,128)}), f32[8,32,56,32]{2,3,1,0:T(8,128)}) %all-gather.6.cloned.1.call-update) | async-done | bytes 1835024 | tf_op jit(solution)/shard_map/all_gather | solution.py:58
  513.4 7.4 %copy.28 = f32[32,4,2,56,32]{3,2,1,0,4:T(2,128)} copy(f32[32,4,2,56,32]{3,4,0,1,2:T(8,128)} %bitcast.53) | data formatting | bytes 3670016 | tf_op jit(solution)/shard_map/transpose | solution.py:61
  520.7 9.2 %reshape_reshape.4 = f32[14336,32]{0,1:T(8,128)} reshape(f32[32,4,2,56,32]{3,2,1,0,4:T(2,128)} %copy.28) | data formatting | bytes 3670016 | tf_op jit(solution)/shard_map/reshape;reshape | solution.py:52
  529.9 0.0 copy-start.2
  529.9 3.2 fusion.16
  533.2 0.0 copy-done.2
  533.2 0.0 copy-start.3
  533.2 1.5 fusion.9
  534.7 0.1 copy-done.3
  (6 shorter events, 0.1 us)
Async XLA Ops:
  7.2 1.5 copy-start
  7.2 10.4 %copy-start.1 = (bf16[1,32,14336]{2,1,0:T(8,128)(2,1)S(1)}, bf16[1,32,14336]{2,1,0:T(8,128)(2,1)}, u32[]{:S(2)}) copy-start(bf16[1,32,14336]{2,1,0:T(8,128)(2,1)} %param.4) | copy-start | bytes 2752516
  12.6 17.8 %all-to-all-start = ((f32[4,1,1024]{2,1,0:T(1,128)}), f32[4,1,1024]{2,1,0:T(1,128)S(1)}, u32[]{:S(2)}, u32[]{:S(2)}) async-start(f32[4,1,1024]{2,1,0:T(1,128)} %reshape.39), calls=%async_computation | async-start | bytes 32768 | tf_op jit(solution)/shard_map/all_to_all | solution.py:12
  17.6 198.8 %reduce-scatter.4.cloned.1.call-start = ((), (), s32[]{:S(2)}) async-start(), calls=%async_computation.5 | async-start | bytes 6291456 | tf_op jit(solution)/shard_map/reduce_scatter | solution.py:34
  191.6 144.6 %reduce-scatter.6.cloned.1.call-start = ((), (), s32[]{:S(2)}) async-start(), calls=%async_computation.6 | async-start | bytes 2162688 | tf_op jit(solution)/shard_map/reduce_scatter | solution.py:34
  216.4 176.2 %reduce-scatter.8.cloned.1.call-start = ((), (), s32[]{:S(2)}) async-start(), calls=%async_computation.7 | async-start | bytes 81920 | tf_op jit(solution)/shard_map/reduce_scatter | solution.py:34
  336.2 177.1 %all-gather.6.cloned.1.call-start = ((), (), s32[]{:S(2)}) async-start(), calls=%async_computation.8 | async-start | bytes 6291456 | tf_op jit(solution)/shard_map/all_gather | solution.py:58
  529.9 3.3 copy-start.2
  533.2 1.5 copy-start.3
Sparse Core Ops, SparseCore 0:
  191.7 24.6 reduce-scatter.3
  219.8 116.3 reduce-scatter.5
  339.6 53.0 reduce-scatter.7
  463.3 50.0 all-gather.5
where the time goes:
time: 542 us; the launch traced here: 541 us
  waiting for transfers between devices  251 us (46%)
  blocking collectives  210 us (39%)
  local copies, waits for them, and re-layouts  33.2 us (6%)
  matrix products  15.3 us (3%)
  between operations  13.9 us (3%)
  other arithmetic  12.2 us (2%)
    reduce_scatter x3, waiting for transfers between devices, own_block(): parts = lax.psum_scatter(parts, axes[k], scatter_dimension=0, tiled=True)  201 us
    psum x3, blocking collectives, over_axes(): array = lax.psum(array, axis)  142 us
    all_gather x2, blocking collectives, gather_in_order(): parts = lax.all_gather(parts, axes[k])  60.8 us
    all_gather x1, waiting for transfers between devices, gather_in_order(): parts = lax.all_gather(parts, axes[k])  50.2 us
  transfers between devices with their start and end apart: 5, of which 4 were waited for; matrix products, arithmetic and copies ran while one was open for 2% of the time, Pallas kernels for 0%

commit v1 on v0

v1 whole, which is shorter than its diff:
```python
import functools

import jax
import jax.numpy as jnp
from jax import lax
from jax.experimental import pallas as pl
from jax.experimental.pallas import tpu as pltpu
from jax.sharding import Mesh
from jax.sharding import PartitionSpec as P

FSDP = ("fsdp_0", "fsdp_1", "fsdp_2")
F32 = jnp.float32
BF16 = jnp.bfloat16
MESH = pl.DeviceIdType.MESH
HIGHEST = lax.Precision.HIGHEST
RANK = 32


def three_parts(v):
    hi = v.astype(BF16)
    rest = v - hi.astype(F32)
    mid = rest.astype(BF16)
    return hi, mid, (rest - mid.astype(F32)).astype(BF16)


def far_first(n):
    return sorted(range(1, n), key=lambda k: -min(k, n - k))


def kernel(
    dims, g_hbm, e_hbm, q_hbm, update_ref, error_ref,
    ge, q0, pslots, core_out, mine, core_in,
    a1, b1, a1s, b1s, a2, b2, zb, z1, f1, zfin, qfin,
    gcore, gx, gz, gf, load_sem, send, recv, hand,
):
    n, zn, far, base = dims
    pieces = 2 * n
    y, z = lax.axis_index("dp"), lax.axis_index("fsdp_0")
    x, c = lax.axis_index("fsdp_1"), lax.axis_index("fsdp_2")
    zc, zi = z // zn, z % zn
    rows = g_hbm.shape[0]
    cols = g_hbm.shape[1]
    width = cols // (2 * pieces)
    lanes = width // 128
    t2 = a2.shape[1]
    zt = z1.shape[1]
    sends = []

    def at_y(k):
        return ((y + k) % n, z, x, c)

    def at_x(k):
        return (y, z, (x + k) % n, c)

    def at_c(k):
        return (y, z, x, (c + k) % 2)

    def at_z(k):
        return (y, zc * zn + (zi + k) % zn, x, c)

    def at_far(k):
        return (y, ((zc + k) % far) * zn + zi, x, c)

    def push(name, src, dst, slot, k, peer):
        copy = pltpu.make_async_remote_copy(
            src_ref=src, dst_ref=dst,
            send_sem=send.at[base[name] + k], recv_sem=recv.at[base[name] + slot],
            device_id=peer, device_id_type=MESH,
        )
        copy.start()
        sends.append(copy)

    def arrive(name, dst, slot):
        pltpu.make_async_remote_copy(
            src_ref=dst, dst_ref=dst,
            send_sem=send.at[base[name]], recv_sem=recv.at[base[name] + slot],
            device_id=at_c(1), device_id_type=MESH,
        ).wait_recv()

    def arrive_all(name, slots, me, count):
        for k in range(1, count):
            at = (me + k) % count
            arrive(name, slots.at[at], at)

    groups = 4
    step = cols // groups
    loads = []
    for i in range(groups):
        part = pl.ds(i * step, step)
        trio = (
            (g_hbm.at[:, part], ge.at[0:rows, part]),
            (e_hbm.at[:, part], ge.at[rows : 2 * rows, part]),
            (q_hbm.at[:, part], q0.at[:, part]),
        )
        trio = [pltpu.make_async_copy(s, d, load_sem.at[i, j]) for j, (s, d) in enumerate(trio)]
        for copy in trio:
            copy.start()
        loads.append(trio)
    barrier = pltpu.get_barrier_semaphore()
    beside = sorted({1, far - 1})
    near = [at_y(k) for k in range(1, n)] + [at_x(k) for k in range(1, n)]
    near += [at_c(1)] + [at_z(k) for k in range(1, zn)] + [at_far(k) for k in beside]
    for peer in near:
        pl.semaphore_signal(barrier, inc=1, device_id=peer, device_id_type=MESH)

    if zn * zt > 2 * t2:
        zb[2 * t2 :] = jnp.zeros((zn * zt - 2 * t2, 8, 128), F32)

    acc = jnp.zeros((2 * rows, 128), F32)
    sub = step // width

    def left(i, acc):
        at = pl.ds(pl.multiple_of(i * width, 128), width)
        q = jnp.concatenate([*three_parts(q0[:, at]), jnp.zeros((RANK, width), BF16)], axis=0)
        return acc + lax.dot_general(
            ge[:, at], q, (((1,), (1,)), ((), ())), preferred_element_type=F32
        )

    for i in range(groups):
        for copy in loads[i]:
            copy.wait()
        acc = lax.fori_loop(i * sub, (i + 1) * sub, left, acc)
    lane = lax.broadcasted_iota(jnp.int32, (rows, 128), 1)
    own = acc[:rows] + acc[rows:]
    own = own + pltpu.roll(own, 96, 1) + pltpu.roll(own, 64, 1)
    pslots[y] = jnp.where(lane < RANK, own, 0.0)

    pl.semaphore_wait(barrier, len(near))
    for k in far_first(n):
        push("p", pslots.at[y], pslots.at[y], y, k, at_y(k))
    if far > 2:
        for k in beside:
            pl.semaphore_signal(hand.at[0], inc=1, device_id=at_far(k), device_id_type=MESH)
    arrive_all("p", pslots, y, n)
    p = pslots[0]
    for k in range(1, n):
        p = p + pslots[k]

    square = jnp.concatenate([p, jnp.zeros((128 - rows, 128), F32)], axis=0)
    turned = square.T[:RANK]
    gram = lax.dot_general(
        turned, square, (((1,), (0,)), ((), ())), precision=HIGHEST, preferred_element_type=F32
    )
    tile = gram[0:8]
    for a in range(1, RANK // 8):
        tile = tile + pltpu.roll(gram[8 * a : 8 * a + 8], 32 * a, 1)
    gcore[c] = tile
    push("gc", gcore.at[c], gcore.at[c], c, 0, at_c(1))

    twice = turned + pltpu.roll(turned, rows, 1)
    p3 = jnp.concatenate([*three_parts(twice)], axis=0)[:, : 2 * rows]

    def right(half, at, out):
        off = pl.multiple_of((half * pieces + at) * width, 128)
        r = lax.dot_general(
            p3, ge[:, pl.ds(off, width)], (((1,), (0,)), ((), ())), preferred_element_type=F32
        )
        r = r[:RANK] + (r[RANK : 2 * RANK] + r[2 * RANK :])
        for j in range(lanes):
            out[at, 4 * j : 4 * j + 4] = r[:, 128 * j : 128 * j + 128].reshape(4, 8, 128)

    order = []
    for k in [*far_first(n), 0]:
        order += [("a", k, (x + k) % n), ("b", k, n + (y + k) % n)]
    for s, (_, _, at) in enumerate(order):
        right((c + 1) % 2, at, core_out)
        push("cr", core_out.at[at], core_in.at[at], s, s, at_c(1))

    arrive("gc", gcore.at[(c + 1) % 2], (c + 1) % 2)
    gx[x] = gcore[0] + gcore[1]
    for k in far_first(n):
        push("gx", gx.at[x], gx.at[x], x, k, at_x(k))
    if far > 4:
        pl.semaphore_wait(hand.at[0], len(beside))
        for k in (2, far - 2):
            pl.semaphore_signal(hand.at[1], inc=1, device_id=at_far(k), device_id_type=MESH)

    for s, (kind, k, at) in enumerate(order):
        right(c, at, mine)
        arrive("cr", core_in.at[at], s)
        mine[at] = mine[at] + core_in[at]
        if k:
            if kind == "a":
                push("a1", mine.at[at], a1.at[x], x, k, at_x(k))
            else:
                push("b1", mine.at[at], b1.at[y], y, k, at_y(k))

    arrive_all("gx", gx, x, n)
    g = gx[0]
    for k in range(1, n):
        g = g + gx[k]
    gz[zi] = g
    for k in range(1, zn):
        push("gz", gz.at[zi], gz.at[zi], zi, k, at_z(k))
    arrive_all("gz", gz, zi, zn)
    g = gz[0]
    for k in range(1, zn):
        g = g + gz[k]
    gf[zc] = g
    if far > 4:
        pl.semaphore_wait(hand.at[1], 2)
    elif far > 2:
        pl.semaphore_wait(hand.at[0], len(beside))
    for k in far_first(far):
        push("gf", gf.at[zc], gf.at[zc], zc, k, at_far(k))

    def gathered(first, slots, me, count):
        total = first
        for k in range(1, count):
            total = total + slots[(me + k) % count]
        return total

    arrive_all("a1", a1, x, n)
    a1s[...] = gathered(mine[x], a1, x, n)
    for k in far_first(n):
        push("a2", a1s.at[pl.ds(((y + k) % n) * t2, t2)], a2.at[y], y, k, at_y(k))
    arrive_all("b1", b1, y, n)
    b1s[...] = gathered(mine[n + y], b1, y, n)
    for k in far_first(n):
        push("b2", b1s.at[pl.ds(((x + k) % n) * t2, t2)], b2.at[x], x, k, at_x(k))
    arrive_all("a2", a2, y, n)
    zb[0:t2] = gathered(a1s[pl.ds(y * t2, t2)], a2, y, n)
    arrive_all("b2", b2, x, n)
    zb[t2 : 2 * t2] = gathered(b1s[pl.ds(x * t2, t2)], b2, x, n)

    for k in range(1, zn):
        push("z1", zb.at[pl.ds(((zi + k) % zn) * zt, zt)], z1.at[zi], zi, k, at_z(k))
    arrive_all("z1", z1, zi, zn)
    f1[zc] = gathered(zb[pl.ds(zi * zt, zt)], z1, zi, zn)
    for k in far_first(far):
        push("f1", f1.at[zc], f1.at[zc], zc, k, at_far(k))

    arrive_all("gf", gf, zc, far)
    g = gf[0]
    for k in range(1, far):
        g = g + gf[k]
    lane = lax.broadcasted_iota(jnp.int32, (RANK, 128), 1)
    line = lax.broadcasted_iota(jnp.int32, (RANK, 128), 0)
    spread = [g] + [pltpu.roll(g, 128 - 32 * a, 1) for a in range(1, RANK // 8)]
    aug = jnp.where(lane < RANK, jnp.concatenate(spread, axis=0), 0.0)
    aug = jnp.where(lane == line + RANK, 1.0, aug)
    for k in range(RANK):
        inv = 1.0 / jnp.sqrt(aug[k : k + 1, k : k + 1])
        row = aug[k : k + 1, :] * inv
        col = aug[:, k : k + 1] * inv
        less = aug - col * row
        aug = jnp.where(line > k, less, jnp.where(line == k, row, aug))
    linv = jnp.where(lane < RANK, pltpu.roll(aug, 96, 1), 0.0)
    linv = jnp.concatenate([linv, jnp.zeros((128 - RANK, 128), F32)], axis=0)
    p_hat = lax.dot_general(
        p, linv, (((1,), (1,)), ((), ())), precision=HIGHEST, preferred_element_type=F32
    )
    w = lax.dot_general(
        p_hat, linv, (((1,), (0,)), ((), ())), precision=HIGHEST, preferred_element_type=F32
    )
    hi, mid, lo = [v.astype(F32) for v in three_parts(w * (1.0 / n))]
    w1 = hi + pltpu.roll(mid, 32, 1) + pltpu.roll(lo, 64, 1) + pltpu.roll(hi, 96, 1)
    w2 = mid + pltpu.roll(hi, 32, 1)
    w6 = jnp.concatenate([w1, w2], axis=1)[:, : 6 * RANK].astype(BF16)

    arrive_all("f1", f1, zc, far)
    total = f1[0]
    for k in range(1, far):
        total = total + f1[k]
    here = pl.ds(zi * zt, zt)
    zfin[here] = total
    for k in range(1, zn):
        push("z2", zfin.at[here], zfin.at[here], zi, k, at_z(k))
    for k in range(1, zn):
        at = (zi + k) % zn
        arrive("z2", zfin.at[pl.ds(at * zt, zt)], at)

    pa, pb = c * pieces + x, c * pieces + n + y
    part_y, part_x = pl.ds(y * t2, t2), pl.ds(x * t2, t2)
    for k in far_first(n):
        push("a3", zfin.at[0:t2], qfin.at[pa, part_y], y, k, at_y(k))
    for k in far_first(n):
        push("b3", zfin.at[t2 : 2 * t2], qfin.at[pb, part_x], x, k, at_x(k))
    qfin[pa, part_y] = zfin[0:t2]
    qfin[pb, part_x] = zfin[t2 : 2 * t2]

    def finish(at):
        q = jnp.concatenate(
            [qfin[at, 4 * j : 4 * j + 4].reshape(RANK, 128) for j in range(lanes)], axis=1
        )
        hi, mid, lo = three_parts(q)
        q6 = jnp.concatenate([hi, hi, hi, mid, mid, lo], axis=0)
        u = lax.dot_general(w6, q6, (((1,), (0,)), ((), ())), preferred_element_type=F32)
        where = pl.ds(pl.multiple_of(at * width, 128), width)
        merged = ge[0:rows, where].astype(F32) + ge[rows : 2 * rows, where].astype(F32)
        update_ref[:, where] = u
        error_ref[:, where] = (merged - u).astype(BF16)

    for k in range(1, n):
        at = (y + k) % n
        arrive("a3", qfin.at[pa, pl.ds(at * t2, t2)], at)
    for k in far_first(n):
        push("a4", qfin.at[pa], qfin.at[pa], x, k, at_x(k))
    push("cg", qfin.at[pa], qfin.at[pa], 0, 0, at_c(1))
    for k in range(1, n):
        at = (x + k) % n
        arrive("b3", qfin.at[pb, pl.ds(at * t2, t2)], at)
    for k in far_first(n):
        push("b4", qfin.at[pb], qfin.at[pb], y, k, at_y(k))
    push("cg", qfin.at[pb], qfin.at[pb], 1, 1, at_c(1))
    finish(pa)
    finish(pb)
    other = (c + 1) % 2
    turns = [x, n + y]
    for k in far_first(n):
        for name, at, slot in (
            ("a4", (x + n - k) % n, (x + n - k) % n),
            ("b4", n + (y + n - k) % n, (y + n - k) % n),
        ):
            s = len(turns)
            turns.append(at)
            at = c * pieces + at
            arrive(name, qfin.at[at], slot)
            push("cg", qfin.at[at], qfin.at[at], s, s, at_c(1))
            finish(at)
    for s, at in enumerate(turns):
        at = other * pieces + at
        arrive("cg", qfin.at[at], s)
        finish(at)
    for copy in sends:
        copy.wait_send()


def body(n, zn, far, grad, error, q_init):
    rows, cols = grad.shape[1:]
    pieces = 2 * n
    t1 = cols // (2 * pieces) // 128 * (RANK // 8)
    t2 = t1 // n
    zt = -(-2 * t2 // zn)
    base, total = {}, 0
    for name, count in (
        ("p", n), ("gc", 2), ("gx", n), ("gz", zn), ("gf", far), ("cr", pieces),
        ("a1", n), ("b1", n), ("a2", n), ("b2", n), ("z1", zn), ("f1", far), ("z2", zn),
        ("a3", n), ("b3", n), ("a4", n), ("b4", n), ("cg", pieces),
    ):
        base[name] = total
        total += count

    def tiles(*lead):
        return pltpu.VMEM((*lead, 8, 128), F32)

    vmem = pl.BlockSpec(memory_space=pltpu.VMEM)
    hbm = pl.BlockSpec(memory_space=pltpu.HBM)
    update, new_error = pl.pallas_call(
        functools.partial(kernel, (n, zn, far, base)),
        out_shape=(
            jax.ShapeDtypeStruct((rows, cols), F32),
            jax.ShapeDtypeStruct((rows, cols), BF16),
        ),
        in_specs=[hbm] * 3,
        out_specs=(vmem, vmem),
        scratch_shapes=[
            pltpu.VMEM((2 * rows, cols), BF16),
            pltpu.VMEM((RANK, cols), F32),
            pltpu.VMEM((n, rows, 128), F32),
            tiles(pieces, t1),
            tiles(pieces, t1),
            tiles(pieces, t1),
            tiles(n, t1),
            tiles(n, t1),
            tiles(t1),
            tiles(t1),
            tiles(n, t2),
            tiles(n, t2),
            tiles(zn * zt),
            tiles(zn, zt),
            tiles(far, zt),
            tiles(zn * zt),
            tiles(2 * pieces, t1),
            tiles(2),
            tiles(n),
            tiles(zn),
            tiles(far),
            pltpu.SemaphoreType.DMA((4, 3)),
            pltpu.SemaphoreType.DMA((total,)),
            pltpu.SemaphoreType.DMA((total,)),
            pltpu.SemaphoreType.REGULAR((2,)),
        ],
        compiler_params=pltpu.CompilerParams(
            collective_id=0, has_side_effects=True, vmem_limit_bytes=60 * 1024 * 1024
        ),
        name="powersgd",
    )(grad[0], error[0], q_init.T)
    return update, new_error[None]


def solution(mesh):
    n, z = mesh.shape["dp"], mesh.shape["fsdp"] // (2 * mesh.shape["dp"])
    zn = min(4, z // 2)
    split = Mesh(mesh.devices.reshape(n, z, n, 2), ("dp", *FSDP))
    placed = (P("dp", FSDP, None), P("dp", FSDP, None), P())
    return jax.shard_map(
        functools.partial(body, n, zn, z // zn),
        mesh=split,
        in_specs=placed,
        out_specs=(P(FSDP, None), P("dp", FSDP, None)),
        check_vma=False,
    )
```

time: 542 us -> 88.3 us (0.16)
  waiting for transfers between devices: 251 us -> 0 us
  blocking collectives: 210 us -> 0 us
  Pallas kernels: 0 us -> 83.6 us
  local copies, waits for them, and re-layouts: 33.2 us -> 3.85 us
  matrix products: 15.3 us -> 0 us
  between operations: 13.9 us -> 0.65 us
  other arithmetic: 12.2 us -> 0 us
    reduce_scatter x3 -> x0, waiting for transfers between devices: 201 us -> none  [own_block(): parts = lax.psum_scatter(parts, axes[k], scatter_dimension=0, tiled=True)]
    psum x3 -> x0, blocking collectives: 142 us -> none  [over_axes(): array = lax.psum(array, axis)]
    pallas_call x0 -> x1, Pallas kernels: none -> 83.6 us  [body(): pl.pallas_call(functools.partial(kernel, (n, zn, far, base)), out_shape=(...]
    all_gather x2 -> x0, blocking collectives: 60.8 us -> none  [gather_in_order(): parts = lax.all_gather(parts, axes[k])]
    all_gather x1 -> x0, waiting for transfers between devices: 50.2 us -> none  [gather_in_order(): parts = lax.all_gather(parts, axes[k])]
    dot_general x4 -> x0, matrix products: 15.1 us -> none  [the longest x1 8.39 us: body(): lax.dot_general(merged, p_hat, (((0,), (0,)), ((), ())), precision=lax.Pr...]
    dot_general x1 -> x0, local copies, waits for them, and re-layouts: 10.2 us -> none  [body(): lax.dot_general(merged, p_hat, (((0,), (0,)), ((), ())), precision=lax.Pr...]
    transpose x2 -> x0, local copies, waits for them, and re-layouts: 9.96 us -> none  [the longest x1 7.39 us: gather_in_order(): parts = parts.transpose(*back, *range(len(axes), parts.ndim))]
  transfers between devices with their start and end apart: 5 -> 0, of which waited for: 4 -> 0; matrix products, arithmetic and copies ran while one was open for 2% -> 0% of each run, Pallas kernels for 0% -> 0%
where the time goes in v1:
time: 88.3 us; the launch traced here: 88.1 us
  Pallas kernels  83.6 us (95%)
  local copies, waits for them, and re-layouts  3.85 us (4%)
    pallas_call x1, Pallas kernels, body(): pl.pallas_call(functools.partial(kernel, (n, zn, far, base)), out_shape=(...  83.6 us
    unnamed x4, local copies, waits for them, and re-layouts  3.85 us

profile of v1, /device:TPU:1, one launch (start us, length us, event | category | flops | bytes accessed | tf_op | source)
XLA Modules:
  0.0 88.1 jit_solution(7558913207481616257)
XLA Ops:
  0.6 83.6 %powersgd.1 = (f32[32,14336]{1,0:T(8,128)}, bf16[32,14336]{1,0:T(8,128)(2,1)}) custom-call(bf16[32,14336]{1,0:T(8,128)(2,1)} %bitcast.5, bf16[32,14336]{1,0:T(8,128)(2,1)} %bitcast.6, f32[32,14336]{1,0:T(8,128)} %bitcast.4), custom_call_target="tpu_custom_call" | custom-call | tf_op jit(solution)/shard_map/powersgd/pallas_call | solution.py:349
  84.2 0.0 copy-start
  84.2 2.9 %copy.7 = f32[32,14336]{1,0:T(8,128)} copy(f32[32,14336]{1,0:T(8,128)} %get-tuple-element.8) | data formatting | bytes 3670016
  87.2 0.0 copy-done
  87.2 0.9 %copy.8 = bf16[1,32,14336]{2,1,0:T(8,128)(2,1)} copy(bf16[1,32,14336]{2,1,0:T(8,128)(2,1)S(1)} %bitcast.7) | data formatting | bytes 1835008
Async XLA Ops:
  84.2 2.9 %copy-start = (bf16[32,14336]{1,0:T(8,128)(2,1)S(1)}, bf16[32,14336]{1,0:T(8,128)(2,1)}, u32[]{:S(2)}) copy-start(bf16[32,14336]{1,0:T(8,128)(2,1)} %get-tuple-element.5) | copy-start | bytes 2752516

commit v2 on v1

v2 whole, which is shorter than its diff:
```python
import functools

import jax
import jax.numpy as jnp
from jax import lax
from jax.experimental import pallas as pl
from jax.experimental.pallas import tpu as pltpu
from jax.sharding import Mesh
from jax.sharding import PartitionSpec as P

FSDP = ("fsdp_0", "fsdp_1", "fsdp_2")
F32 = jnp.float32
BF16 = jnp.bfloat16
MESH = pl.DeviceIdType.MESH
HIGHEST = lax.Precision.HIGHEST
RANK = 32
PARTS = 4
GRANT = 52200


def three_parts(v):
    hi = v.astype(BF16)
    rest = v - hi.astype(F32)
    mid = rest.astype(BF16)
    return hi, mid, (rest - mid.astype(F32)).astype(BF16)


def far_first(n):
    return sorted(range(1, n), key=lambda k: -min(k, n - k))


def pack(v):
    tile = v[0:8]
    for a in range(1, RANK // 8):
        tile = tile + pltpu.roll(v[8 * a : 8 * a + 8], RANK * a, 1)
    return tile


def unpack(tile):
    spread = [tile] + [pltpu.roll(tile, 128 - RANK * a, 1) for a in range(1, RANK // 8)]
    lane = lax.broadcasted_iota(jnp.int32, (RANK, 128), 1)
    return jnp.where(lane < RANK, jnp.concatenate(spread, axis=0), 0.0)


def kernel(
    dims, g_hbm, e_hbm, q_hbm, *refs
):
    n, zn, far, base, parts = dims
    update_refs, error_ref, refs = refs[:parts], refs[parts], refs[parts + 1 :]
    (
        ge, q0, pslots, core_out, mine, core_in,
        a1, b1, a1s, b1s, a2, b2, f1, zfin, afin, bfin, qfin,
        gcore, gx, gz, gf, load_sem, send, recv, hand,
    ) = refs
    pieces = 2 * n
    y, z = lax.axis_index("dp"), lax.axis_index("fsdp_0")
    x, c = lax.axis_index("fsdp_1"), lax.axis_index("fsdp_2")
    zc, zi = z // zn, z % zn
    rows = g_hbm.shape[0]
    cols = g_hbm.shape[1]
    width = cols // (2 * pieces)
    lanes = width // 128
    t1 = mine.shape[1]
    t2 = t1 // n
    t3 = a2.shape[2]
    sends = []
    sent = iter(range(send.shape[0]))

    def at(dy=0, dx=0, dc=0, dz=0, df=0):
        to_y = (y + dy) % n if dy else y
        to_x = (x + dx) % n if dx else x
        to_c = (c + dc) % 2 if dc else c
        to_zi = (zi + dz) % zn if dz else zi
        to_zc = (zc + df) % far if df else zc
        return (to_y, to_zc * zn + to_zi, to_x, to_c)

    def push(name, src, dst, slot, peer):
        copy = pltpu.make_async_remote_copy(
            src_ref=src, dst_ref=dst,
            send_sem=send.at[next(sent)], recv_sem=recv.at[base[name] + slot],
            device_id=peer, device_id_type=MESH,
        )
        copy.start()
        sends.append(copy)

    def arrive(name, dst, slot):
        pltpu.make_async_remote_copy(
            src_ref=dst, dst_ref=dst,
            send_sem=send.at[0], recv_sem=recv.at[base[name] + slot],
            device_id=at(dc=1), device_id_type=MESH,
        ).wait_recv()

    def arrive_all(name, slots, me, count):
        for k in range(1, count):
            src = (me + k) % count
            arrive(name, slots.at[src], src)

    groups = 4
    step = cols // groups
    loads = []
    for i in range(groups):
        part = pl.ds(i * step, step)
        trio = (
            (g_hbm.at[:, part], ge.at[0:rows, part]),
            (e_hbm.at[:, part], ge.at[rows : 2 * rows, part]),
            (q_hbm.at[:, part], q0.at[:, part]),
        )
        trio = [pltpu.make_async_copy(s, d, load_sem.at[i, j]) for j, (s, d) in enumerate(trio)]
        for copy in trio:
            copy.start()
        loads.append(trio)
    barrier = pltpu.get_barrier_semaphore()
    beside = sorted({1, far - 1})
    near = [at(dy=k, dz=m) for m in range(zn) for k in range(n) if k or m]
    near += [at(dx=k, dz=m) for m in range(zn) for k in range(1, n)]
    near += [at(dc=1)] + [at(df=k) for k in beside]
    for peer in near:
        pl.semaphore_signal(barrier, inc=1, device_id=peer, device_id_type=MESH)

    for k in range(n if zn * t3 > t2 else 0):
        a1s[k, t2:] = jnp.zeros((zn * t3 - t2, 8, 128), F32)
        b1s[k, t2:] = jnp.zeros((zn * t3 - t2, 8, 128), F32)

    acc = jnp.zeros((2 * rows, 128), F32)
    sub = step // width

    def left(i, acc):
        where = pl.ds(pl.multiple_of(i * width, 128), width)
        q = jnp.concatenate([*three_parts(q0[:, where]), jnp.zeros((RANK, width), BF16)], axis=0)
        return acc + lax.dot_general(
            ge[:, where], q, (((1,), (1,)), ((), ())), preferred_element_type=F32
        )

    for i in range(groups):
        for copy in loads[i]:
            copy.wait()
        acc = lax.fori_loop(i * sub, (i + 1) * sub, left, acc)
    lane = lax.broadcasted_iota(jnp.int32, (rows, 128), 1)
    own = acc[:rows] + acc[rows:]
    own = own + pltpu.roll(own, 96, 1) + pltpu.roll(own, 64, 1)
    pslots[y] = pack(jnp.where(lane < RANK, own, 0.0))

    pl.semaphore_wait(barrier, len(near))
    for k in far_first(n):
        push("p", pslots.at[y], pslots.at[y], y, at(dy=k))
    if far > 2:
        for k in beside:
            pl.semaphore_signal(hand.at[0], inc=1, device_id=at(df=k), device_id_type=MESH)
    arrive_all("p", pslots, y, n)
    p = pslots[0]
    for k in range(1, n):
        p = p + pslots[k]
    p = unpack(p)

    square = jnp.concatenate([p, jnp.zeros((128 - rows, 128), F32)], axis=0)
    turned = square.T[:RANK]
    gram = lax.dot_general(
        turned, square, (((1,), (0,)), ((), ())), precision=HIGHEST, preferred_element_type=F32
    )
    gcore[c] = pack(gram)
    push("gc", gcore.at[c], gcore.at[c], c, at(dc=1))

    twice = turned + pltpu.roll(turned, rows, 1)
    p3 = jnp.concatenate([*three_parts(twice)], axis=0)[:, : 2 * rows]

    def right(half, piece):
        off = pl.multiple_of((half * pieces + piece) * width, 128)
        r = lax.dot_general(
            p3, ge[:, pl.ds(off, width)], (((1,), (0,)), ((), ())), preferred_element_type=F32
        )
        r = r[:RANK] + (r[RANK : 2 * RANK] + r[2 * RANK :])
        return [r[:, 128 * j : 128 * j + 128].reshape(4, 8, 128) for j in range(lanes)]

    order = []
    for k in [*far_first(n), 0]:
        order += [("a", k, (x + k) % n), ("b", k, n + (y + k) % n)]
    turn = [*far_first(n), 0]

    def first_stage(kind, k, piece, group):
        if kind == "a":
            g = (y + group) % n
            part = pl.ds(g * t2, t2)
            push("a1", mine.at[piece, part], a1.at[x, part], x * n + g, at(dx=k))
        else:
            g = (x + group) % n
            part = pl.ds(g * t2, t2)
            push("b1", mine.at[piece, part], b1.at[y, part], y * n + g, at(dy=k))

    ahead = 3
    for s in range(len(order) + ahead):
        if s < len(order):
            piece = order[s][2]
            for j, tile in enumerate(right((c + 1) % 2, piece)):
                core_out[piece, 4 * j : 4 * j + 4] = tile
            push("cr", core_out.at[piece], core_in.at[piece], s, at(dc=1))
        if s == 5:
            arrive("gc", gcore.at[(c + 1) % 2], (c + 1) % 2)
            gx[x] = gcore[0] + gcore[1]
            for k in far_first(n):
                push("gx", gx.at[x], gx.at[x], x, at(dx=k))
            if far > 4:
                pl.semaphore_wait(hand.at[0], len(beside))
                for k in (2, far - 2):
                    pl.semaphore_signal(
                        hand.at[1], inc=1, device_id=at(df=k), device_id_type=MESH
                    )
        if s >= ahead:
            kind, k, piece = order[s - ahead]
            tiles = right(c, piece)
            arrive("cr", core_in.at[piece], s - ahead)
            for j, tile in enumerate(tiles):
                part = slice(4 * j, 4 * j + 4)
                mine[piece, part] = tile + core_in[piece, part]
            if k:
                for group in turn[: n // 2]:
                    first_stage(kind, k, piece, group)
    for group in turn[n // 2 :]:
        for kind, k, piece in order:
            if k:
                first_stage(kind, k, piece, group)

    arrive_all("gx", gx, x, n)
    g = gx[0]
    for k in range(1, n):
        g = g + gx[k]
    gz[zi] = g
    for k in range(1, zn):
        push("gz", gz.at[zi], gz.at[zi], zi, at(dz=k))

    for group in turn:
        for kind in ("a", "b"):
            if kind == "a":
                me, other, slots, sums, piece = x, y, a1, a1s, x
            else:
                me, other, slots, sums, piece = y, x, b1, b1s, n + y
            g = (other + group) % n
            part = pl.ds(g * t2, t2)
            total = mine[piece, part]
            for k in range(1, n):
                src = (me + k) % n
                arrive(kind + "1", slots.at[src, part], src * n + g)
                total = total + slots[src, part]
            sums[g, 0:t2] = total
            for m in range(zn):
                if group == 0 and m == 0:
                    continue
                chunk = sums.at[g, pl.ds(((zi + m) % zn) * t3, t3)]
                slot = other * zn + zi
                if kind == "a":
                    push("a2", chunk, a2.at[y, zi], slot, at(dy=group, dz=m))
                else:
                    push("b2", chunk, b2.at[x, zi], slot, at(dx=group, dz=m))

    arrive_all("gz", gz, zi, zn)
    g = gz[0]
    for k in range(1, zn):
        g = g + gz[k]
    gf[zc] = g
    if far > 4:
        pl.semaphore_wait(hand.at[1], 2)
    elif far > 2:
        pl.semaphore_wait(hand.at[0], len(beside))
    for k in far_first(far):
        push("gf", gf.at[zc], gf.at[zc], zc, at(df=k))

    own_part = pl.ds(zi * t3, t3)
    for kind in ("a", "b"):
        other, slots, sums = (y, a2, a1s) if kind == "a" else (x, b2, b1s)
        total = sums[other, own_part]
        for group in [0, *far_first(n)[::-1]]:
            for m in range(zn):
                if group == 0 and m == 0:
                    continue
                o, i = (other + group) % n, (zi + m) % zn
                arrive(kind + "2", slots.at[o, i], o * zn + i)
                total = total + slots[o, i]
        if kind == "a":
            f1[zc, 0:t3] = total
        else:
            f1[zc, t3:] = total

    for k in far_first(far):
        push("f1", f1.at[zc], f1.at[zc], zc, at(df=k))

    arrive_all("gf", gf, zc, far)
    g = gf[0]
    for k in range(1, far):
        g = g + gf[k]
    lane = lax.broadcasted_iota(jnp.int32, (RANK, 128), 1)
    line = lax.broadcasted_iota(jnp.int32, (RANK, 128), 0)
    aug = jnp.where(lane == line + RANK, 1.0, unpack(g))
    for k in range(RANK):
        inv = 1.0 / jnp.sqrt(aug[k : k + 1, k : k + 1])
        row = aug[k : k + 1, :] * inv
        col = aug[:, k : k + 1] * inv
        less = aug - col * row
        aug = jnp.where(line > k, less, jnp.where(line == k, row, aug))
    linv = jnp.where(lane < RANK, pltpu.roll(aug, 96, 1), 0.0)
    linv = jnp.concatenate([linv, jnp.zeros((128 - RANK, 128), F32)], axis=0)
    p_hat = lax.dot_general(
        p, linv, (((1,), (1,)), ((), ())), precision=HIGHEST, preferred_element_type=F32
    )
    w = lax.dot_general(
        p_hat, linv, (((1,), (0,)), ((), ())), precision=HIGHEST, preferred_element_type=F32
    )
    hi, mid, lo = [v.astype(F32) for v in three_parts(w * (1.0 / n))]
    w1 = hi + pltpu.roll(mid, 32, 1) + pltpu.roll(lo, 64, 1) + pltpu.roll(hi, 96, 1)
    w2 = mid + pltpu.roll(hi, 32, 1)
    w6 = jnp.concatenate([w1, w2], axis=1)[:, : 6 * RANK].astype(BF16)

    arrive_all("f1", f1, zc, far)
    total = f1[0]
    for k in range(1, far):
        total = total + f1[k]
    zfin[...] = total

    for group in turn:
        for m in range(zn):
            if group == 0 and m == 0:
                continue
            slot = zi + zn * y
            push("a3", zfin.at[0:t3], afin.at[y, own_part], slot, at(dy=group, dz=m))
            slot = zi + zn * x
            push("b3", zfin.at[t3 : 2 * t3], bfin.at[x, own_part], slot, at(dx=group, dz=m))
    afin[y, own_part] = total[:t3]
    bfin[x, own_part] = total[t3:]

    def finish(piece):
        q = jnp.concatenate(
            [qfin[piece, 4 * j : 4 * j + 4].reshape(RANK, 128) for j in range(lanes)], axis=1
        )
        hi, mid, lo = three_parts(q)
        q6 = jnp.concatenate([hi, hi, hi, mid, mid, lo], axis=0)
        u = lax.dot_general(w6, q6, (((1,), (0,)), ((), ())), preferred_element_type=F32)
        where = pl.ds(pl.multiple_of(piece * width, 128), width)
        merged = ge[0:rows, where].astype(F32) + ge[rows : 2 * rows, where].astype(F32)
        lines = rows // parts
        for i in range(parts):
            update_refs[i][:, where] = u[i * lines : i * lines + lines]
        error_ref[:, where] = (merged - u).astype(BF16)

    pa, pb = c * pieces + x, c * pieces + n + y
    for group in turn[::-1]:
        for kind in ("a", "b"):
            other, slots, piece = (y, afin, pa) if kind == "a" else (x, bfin, pb)
            g = (other + group) % n
            for m in range(zn):
                if group == 0 and m == 0:
                    continue
                i = (zi + m) % zn
                arrive(kind + "3", slots.at[g, pl.ds(i * t3, t3)], g * zn + i)
            part = pl.ds(g * t2, t2)
            for k in far_first(n):
                if kind == "a":
                    push("a4", afin.at[g, 0:t2], qfin.at[pa, part], x * n + g, at(dx=k))
                else:
                    push("b4", bfin.at[g, 0:t2], qfin.at[pb, part], y * n + g, at(dy=k))
            slot = (0 if kind == "a" else n) + g
            push("cg", slots.at[g, 0:t2], qfin.at[piece, part], slot, at(dc=1))
            qfin[piece, part] = slots[g, 0:t2]

    finish(pa)
    finish(pb)
    half = c * pieces
    turns = []
    for k in far_first(n):
        for name, src, piece in (
            ("a4", (x + n - k) % n, (x + n - k) % n),
            ("b4", (y + n - k) % n, n + (y + n - k) % n),
        ):
            for group in turn[::-1]:
                g = ((y if name == "a4" else x) + group) % n
                arrive(name, qfin.at[half + piece, pl.ds(g * t2, t2)], src * n + g)
            push("ch", qfin.at[half + piece], qfin.at[half + piece], len(turns), at(dc=1))
            turns.append(piece)
            finish(half + piece)
    half = ((c + 1) % 2) * pieces
    for piece, slot in ((x, 0), (n + y, n)):
        for g in range(n):
            arrive("cg", qfin.at[half + piece, g * t2 : g * t2 + t2], slot + g)
        finish(half + piece)
    for s, piece in enumerate(turns):
        arrive("ch", qfin.at[half + piece], s)
        finish(half + piece)
    for copy in sends:
        copy.wait_send()


def body(n, zn, far, grad, error, q_init):
    rows, cols = grad.shape[1:]
    pieces = 2 * n
    t1 = cols // (2 * pieces) // 128 * (RANK // 8)
    t2 = t1 // n
    t3 = -(-t2 // zn)
    base, total = {}, 0
    for name, count in (
        ("p", n), ("gc", 2), ("gx", n), ("gz", zn), ("gf", far), ("cr", pieces),
        ("a1", n * n), ("b1", n * n), ("a2", n * zn), ("b2", n * zn), ("f1", far),
        ("a3", n * zn), ("b3", n * zn), ("a4", n * n), ("b4", n * n),
        ("cg", pieces), ("ch", pieces),
    ):
        base[name] = total
        total += count

    def tiles(*lead):
        return pltpu.VMEM((*lead, 8, 128), F32)

    vmem = pl.BlockSpec(memory_space=pltpu.VMEM)
    hbm = pl.BlockSpec(memory_space=pltpu.HBM)
    parts = PARTS
    *update, new_error = pl.pallas_call(
        functools.partial(kernel, (n, zn, far, base, parts)),
        out_shape=(
            *[jax.ShapeDtypeStruct((rows // parts, cols), F32)] * parts,
            jax.ShapeDtypeStruct((rows, cols), BF16),
        ),
        in_specs=[hbm] * 3,
        out_specs=(vmem,) * (parts + 1),
        scratch_shapes=[
            pltpu.VMEM((2 * rows, cols), BF16),
            pltpu.VMEM((RANK, cols), F32),
            tiles(n),
            tiles(pieces, t1),
            tiles(pieces, t1),
            tiles(pieces, t1),
            tiles(n, t1),
            tiles(n, t1),
            tiles(n, zn * t3),
            tiles(n, zn * t3),
            tiles(n, zn, t3),
            tiles(n, zn, t3),
            tiles(far, 2 * t3),
            tiles(2 * t3),
            tiles(n, zn * t3),
            tiles(n, zn * t3),
            tiles(2 * pieces, t1),
            tiles(2),
            tiles(n),
            tiles(zn),
            tiles(far),
            pltpu.SemaphoreType.DMA((4, 3)),
            pltpu.SemaphoreType.DMA((total,)),
            pltpu.SemaphoreType.DMA((total,)),
            pltpu.SemaphoreType.REGULAR((2,)),
        ],
        compiler_params=pltpu.CompilerParams(
            collective_id=0, has_side_effects=True, vmem_limit_bytes=GRANT * 1024
        ),
        name="powersgd",
    )(grad[0], error[0], q_init.T)
    return jnp.concatenate(update, axis=0), new_error[None]


def solution(mesh):
    n, z = mesh.shape["dp"], mesh.shape["fsdp"] // (2 * mesh.shape["dp"])
    zn = min(4, z // 2)
    split = Mesh(mesh.devices.reshape(n, z, n, 2), ("dp", *FSDP))
    placed = (P("dp", FSDP, None), P("dp", FSDP, None), P())
    return jax.shard_map(
        functools.partial(body, n, zn, z // zn),
        mesh=split,
        in_specs=placed,
        out_specs=(P(FSDP, None), P("dp", FSDP, None)),
        check_vma=False,
    )
```

time: 88.3 us -> 85.6 us (0.969)
  local copies, waits for them, and re-layouts: 3.85 us -> 0.92 us
  other arithmetic: 0 us -> 1.35 us
  Pallas kernels: 83.6 us -> 82.5 us
    unnamed x4 -> x1, local copies, waits for them, and re-layouts: 3.85 us -> 0.92 us
    concatenate x0 -> x1, other arithmetic: none -> 1.35 us  [body(): return (jnp.concatenate(update, axis=0), new_error[None])]
    pallas_call x1, Pallas kernels: 83.6 us -> 82.5 us  [body(): pl.pallas_call(functools.partial(kernel, (n, zn, far, base, parts)), out_...]
where the time goes in v2:
time: 85.6 us; the launch traced here: 85.4 us
  Pallas kernels  82.5 us (96%)
  other arithmetic  1.35 us (2%)
  local copies, waits for them, and re-layouts  0.92 us (1%)
    pallas_call x1, Pallas kernels, body(): pl.pallas_call(functools.partial(kernel, (n, zn, far, base, parts)), out_...  82.5 us

profile of v2, /device:TPU:1, one launch (start us, length us, event | category | flops | bytes accessed | tf_op | source)
XLA Modules:
  0.0 85.4 jit_solution(4059494775388437929)
XLA Ops:
  0.6 82.5 %powersgd.1 = (f32[8,14336]{1,0:T(8,128)S(1)}, f32[8,14336]{1,0:T(8,128)S(1)}, f32[8,14336]{1,0:T(8,128)S(1)}, f32[8,14336]{1,0:T(8,128)S(1)}, bf16[32,14336]{1,0:T(8,128)(2,1)S(1)}) custom-call(bf16[32,14336]{1,0:T(8,128)(2,1)} %bitcast.6, bf16[32,14336]{1,0:T(8,128)(2,1)} %bitcast.7, f32[32,14336]{1,0:T(8,128)} %bitcast.5), custom_call_target="tpu_custom_call" | custom-call | tf_op jit(solution)/shard_map/powersgd/pallas_call | solution.py:411
  83.2 1.3 %pad_maximum_fusion = f32[32,14336]{1,0:T(8,128)} fusion(f32[8,14336]{1,0:T(8,128)S(1)} %get-tuple-element.10, f32[8,14336]{1,0:T(8,128)S(1)} %get-tuple-element.9, f32[8,14336]{1,0:T(8,128)S(1)} %get-tuple-element.8, f32[8,14336]{1,0:T(8,128)S(1)} %get-tuple-element.7), kind=kLoop, calls=%fused_computation | loop fusion | flops 1376256 | bytes 3670016 | tf_op jit(solution)/shard_map/concatenate | solution.py:451
  84.5 0.9 %copy.6 = bf16[1,32,14336]{2,1,0:T(8,128)(2,1)} copy(bf16[1,32,14336]{2,1,0:T(8,128)(2,1)S(1)} %bitcast.4) | data formatting | bytes 1835008

commit v3 on v2

--- a/solution.py
+++ b/solution.py
@@ -50,7 +50,7 @@
     (
         ge, q0, pslots, core_out, mine, core_in,
         a1, b1, a1s, b1s, a2, b2, f1, zfin, afin, bfin, qfin,
-        gcore, gx, gz, gf, load_sem, send, recv, hand,
+        gcore, gx, gf, load_sem, send, recv, hand,
     ) = refs
     pieces = 2 * n
     y, z = lax.axis_index("dp"), lax.axis_index("fsdp_0")
@@ -122,19 +122,16 @@
         b1s[k, t2:] = jnp.zeros((zn * t3 - t2, 8, 128), F32)
 
     acc = jnp.zeros((2 * rows, 128), F32)
-    sub = step // width
-
-    def left(i, acc):
-        where = pl.ds(pl.multiple_of(i * width, 128), width)
-        q = jnp.concatenate([*three_parts(q0[:, where]), jnp.zeros((RANK, width), BF16)], axis=0)
-        return acc + lax.dot_general(
-            ge[:, where], q, (((1,), (1,)), ((), ())), preferred_element_type=F32
-        )
-
+    sub = step // 2
     for i in range(groups):
         for copy in loads[i]:
             copy.wait()
-        acc = lax.fori_loop(i * sub, (i + 1) * sub, left, acc)
+        for j in range(i * step, (i + 1) * step, sub):
+            q = [*three_parts(q0[:, j : j + sub]), jnp.zeros((RANK, sub), BF16)]
+            acc = acc + lax.dot_general(
+                ge[:, j : j + sub], jnp.concatenate(q, axis=0),
+                (((1,), (1,)), ((), ())), preferred_element_type=F32,
+            )
     lane = lax.broadcasted_iota(jnp.int32, (rows, 128), 1)
     own = acc[:rows] + acc[rows:]
     own = own + pltpu.roll(own, 96, 1) + pltpu.roll(own, 64, 1)
@@ -193,11 +190,13 @@
             for j, tile in enumerate(right((c + 1) % 2, piece)):
                 core_out[piece, 4 * j : 4 * j + 4] = tile
             push("cr", core_out.at[piece], core_in.at[piece], s, at(dc=1))
-        if s == 5:
+        if s == 4:
             arrive("gc", gcore.at[(c + 1) % 2], (c + 1) % 2)
-            gx[x] = gcore[0] + gcore[1]
-            for k in far_first(n):
-                push("gx", gx.at[x], gx.at[x], x, at(dx=k))
+            gx[x, zi] = gcore[0] + gcore[1]
+            for k in turn:
+                for m in range(zn):
+                    if k or m:
+                        push("gx", gx.at[x, zi], gx.at[x, zi], x * zn + zi, at(dx=k, dz=m))
             if far > 4:
                 pl.semaphore_wait(hand.at[0], len(beside))
                 for k in (2, far - 2):
@@ -214,20 +213,31 @@
             if k:
                 for group in turn[: n // 2]:
                     first_stage(kind, k, piece, group)
-    for group in turn[n // 2 :]:
-        for kind, k, piece in order:
-            if k:
-                first_stage(kind, k, piece, group)
-
-    arrive_all("gx", gx, x, n)
-    g = gx[0]
-    for k in range(1, n):
-        g = g + gx[k]
-    gz[zi] = g
-    for k in range(1, zn):
-        push("gz", gz.at[zi], gz.at[zi], zi, at(dz=k))
+            if s - ahead == 2 * (n - 1) - 1:
+                for group in turn[n // 2 :]:
+                    for entry in order[: 2 * (n - 1)]:
+                        first_stage(*entry, group)
+
+    def gram_far():
+        for k in range(n):
+            for m in range(zn):
+                if k or m:
+                    i, j = (x + k) % n, (zi + m) % zn
+                    arrive("gx", gx.at[i, j], i * zn + j)
+        total = gx[0, 0]
+        for i in range(1, n * zn):
+            total = total + gx[i // zn, i % zn]
+        gf[zc] = total
+        if far > 4:
+            pl.semaphore_wait(hand.at[1], 2)
+        elif far > 2:
+            pl.semaphore_wait(hand.at[0], len(beside))
+        for k in far_first(far):
+            push("gf", gf.at[zc], gf.at[zc], zc, at(df=k))
 
     for group in turn:
+        if group == turn[n // 2]:
+            gram_far()
         for kind in ("a", "b"):
             if kind == "a":
                 me, other, slots, sums, piece = x, y, a1, a1s, x
@@ -250,18 +260,6 @@
                     push("a2", chunk, a2.at[y, zi], slot, at(dy=group, dz=m))
                 else:
                     push("b2", chunk, b2.at[x, zi], slot, at(dx=group, dz=m))
-
-    arrive_all("gz", gz, zi, zn)
-    g = gz[0]
-    for k in range(1, zn):
-        g = g + gz[k]
-    gf[zc] = g
-    if far > 4:
-        pl.semaphore_wait(hand.at[1], 2)
-    elif far > 2:
-        pl.semaphore_wait(hand.at[0], len(beside))
-    for k in far_first(far):
-        push("gf", gf.at[zc], gf.at[zc], zc, at(df=k))
 
     own_part = pl.ds(zi * t3, t3)
     for kind in ("a", "b"):
@@ -314,7 +312,7 @@
         total = total + f1[k]
     zfin[...] = total
 
-    for group in turn:
+    for group in turn[::-1]:
         for m in range(zn):
             if group == 0 and m == 0:
                 continue
@@ -386,6 +384,20 @@
         copy.wait_send()
 
 
+def write_out(*refs):
+    *parts, error, whole, rounded, sem = refs
+    lines = parts[0].shape[0]
+    copies = [
+        pltpu.make_async_copy(part, whole.at[i * lines : i * lines + lines], sem.at[i])
+        for i, part in enumerate(parts)
+    ]
+    copies.append(pltpu.make_async_copy(error, rounded, sem.at[len(parts)]))
+    for copy in copies:
+        copy.start()
+    for copy in copies:
+        copy.wait()
+
+
 def body(n, zn, far, grad, error, q_init):
     rows, cols = grad.shape[1:]
     pieces = 2 * n
@@ -394,7 +406,7 @@
     t3 = -(-t2 // zn)
     base, total = {}, 0
     for name, count in (
-        ("p", n), ("gc", 2), ("gx", n), ("gz", zn), ("gf", far), ("cr", pieces),
+        ("p", n), ("gc", 2), ("gx", n * zn), ("gf", far), ("cr", pieces),
         ("a1", n * n), ("b1", n * n), ("a2", n * zn), ("b2", n * zn), ("f1", far),
         ("a3", n * zn), ("b3", n * zn), ("a4", n * n), ("b4", n * n),
         ("cg", pieces), ("ch", pieces),
@@ -435,8 +447,7 @@
             tiles(n, zn * t3),
             tiles(2 * pieces, t1),
             tiles(2),
-            tiles(n),
-            tiles(zn),
+            tiles(n, zn),
             tiles(far),
             pltpu.SemaphoreType.DMA((4, 3)),
             pltpu.SemaphoreType.DMA((total,)),
@@ -448,7 +459,19 @@
         ),
         name="powersgd",
     )(grad[0], error[0], q_init.T)
-    return jnp.concatenate(update, axis=0), new_error[None]
+    whole, rounded = pl.pallas_call(
+        write_out,
+        out_shape=(
+            jax.ShapeDtypeStruct((rows, cols), F32),
+            jax.ShapeDtypeStruct((rows, cols), BF16),
+        ),
+        in_specs=[vmem] * (parts + 1),
+        out_specs=(hbm, hbm),
+        scratch_shapes=[pltpu.SemaphoreType.DMA((parts + 1,))],
+        compiler_params=pltpu.CompilerParams(vmem_limit_bytes=1024 * 1024),
+        name="write_out",
+    )(*update, new_error)
+    return whole, rounded[None]
 
 
 def solution(mesh):

time: 85.6 us -> 85.1 us (level)
  Pallas kernels: 82.5 us -> 84.3 us
  other arithmetic: 1.35 us -> 0 us
  local copies, waits for them, and re-layouts: 0.92 us -> 0 us
    pallas_call x0 -> x1, Pallas kernels: none -> 1.57 us  [body(): pl.pallas_call(write_out, out_shape=(jax.ShapeDtypeStruct((rows, cols), F...]
    concatenate x1 -> x0, other arithmetic: 1.35 us -> none  [body(): return (jnp.concatenate(update, axis=0), new_error[None])]
    unnamed x1 -> x0, local copies, waits for them, and re-layouts: 0.92 us -> none
where the time goes in v3:
time: 85.1 us; the launch traced here: 84.9 us
  Pallas kernels  84.3 us (99%)
    pallas_call x1, Pallas kernels, body(): pl.pallas_call(functools.partial(kernel, (n, zn, far, base, parts)), out_...  82.7 us

profile of v3, /device:TPU:1, one launch (start us, length us, event | category | flops | bytes accessed | tf_op | source)
XLA Modules:
  0.0 84.9 jit_solution(7811503658516972217)
XLA Ops:
  0.6 82.7 %powersgd.1 = (f32[8,14336]{1,0:T(8,128)S(1)}, f32[8,14336]{1,0:T(8,128)S(1)}, f32[8,14336]{1,0:T(8,128)S(1)}, f32[8,14336]{1,0:T(8,128)S(1)}, bf16[32,14336]{1,0:T(8,128)(2,1)S(1)}) custom-call(bf16[32,14336]{1,0:T(8,128)(2,1)} %bitcast.5, bf16[32,14336]{1,0:T(8,128)(2,1)} %bitcast.6, f32[32,14336]{1,0:T(8,128)} %bitcast.4), custom_call_target="tpu_custom_call" | custom-call | tf_op jit(solution)/shard_map/powersgd/pallas_call | solution.py:423
  83.3 1.6 %write_out.1 = (f32[32,14336]{1,0:T(8,128)}, bf16[32,14336]{1,0:T(8,128)(2,1)}) custom-call(f32[8,14336]{1,0:T(8,128)S(1)} %get-tuple-element.9.refs_0_, f32[8,14336]{1,0:T(8,128)S(1)} %get-tuple-element.10.refs_1_, f32[8,14336]{1,0:T(8,128)S(1)} %get-tuple-element.11.refs_2_, f32[8,14336]{1,0:T(8,128)S(1)} %get-tuple-element.12.refs_3_, ...), custom_call_target="tpu_custom_call" | custom-call | tf_op jit(solution)/shard_map/write_out/pallas_call | solution.py:462

commit v4 on v3

--- a/solution.py
+++ b/solution.py
@@ -113,9 +113,24 @@
     beside = sorted({1, far - 1})
     near = [at(dy=k, dz=m) for m in range(zn) for k in range(n) if k or m]
     near += [at(dx=k, dz=m) for m in range(zn) for k in range(1, n)]
-    near += [at(dc=1)] + [at(df=k) for k in beside]
+    near += [at(dc=1)]
+    first, last = zi == 0, zi == zn - 1
+    below = (y, (z + zn * far - 1) % (zn * far), x, c)
+    above = (y, (z + 1) % (zn * far), x, c)
+
+    def tell(sem, peer):
+        pl.semaphore_signal(sem, inc=1, device_id=peer, device_id_type=MESH)
+
+    @pl.when(first)
+    def _():
+        tell(barrier, below)
+
+    @pl.when(last)
+    def _():
+        tell(barrier, above)
+
     for peer in near:
-        pl.semaphore_signal(barrier, inc=1, device_id=peer, device_id_type=MESH)
+        tell(barrier, peer)
 
     for k in range(n if zn * t3 > t2 else 0):
         a1s[k, t2:] = jnp.zeros((zn * t3 - t2, 8, 128), F32)
@@ -137,13 +152,27 @@
     own = own + pltpu.roll(own, 96, 1) + pltpu.roll(own, 64, 1)
     pslots[y] = pack(jnp.where(lane < RANK, own, 0.0))
 
-    pl.semaphore_wait(barrier, len(near))
+    edge = jnp.where(first, 1, 0) + jnp.where(last, 1, 0)
+    pl.semaphore_wait(barrier, len(near) + edge)
+
+    @pl.when(first)
+    def _():
+        tell(hand.at[2], below)
+
+    @pl.when(last)
+    def _():
+        tell(hand.at[2], above)
+
     for k in far_first(n):
         push("p", pslots.at[y], pslots.at[y], y, at(dy=k))
-    if far > 2:
-        for k in beside:
-            pl.semaphore_signal(hand.at[0], inc=1, device_id=at(df=k), device_id_type=MESH)
     arrive_all("p", pslots, y, n)
+
+    @pl.when(first | last)
+    def _():
+        pl.semaphore_wait(hand.at[2], 1)
+        for k in range(1, zn):
+            tell(hand.at[3], at(dz=k))
+
     p = pslots[0]
     for k in range(1, n):
         p = p + pslots[k]
@@ -197,12 +226,10 @@
                 for m in range(zn):
                     if k or m:
                         push("gx", gx.at[x, zi], gx.at[x, zi], x * zn + zi, at(dx=k, dz=m))
-            if far > 4:
-                pl.semaphore_wait(hand.at[0], len(beside))
-                for k in (2, far - 2):
-                    pl.semaphore_signal(
-                        hand.at[1], inc=1, device_id=at(df=k), device_id_type=MESH
-                    )
+            pl.semaphore_wait(hand.at[3], 2 - edge)
+            if far > 2:
+                for k in beside:
+                    tell(hand.at[0], at(df=k))
         if s >= ahead:
             kind, k, piece = order[s - ahead]
             tiles = right(c, piece)
@@ -218,6 +245,30 @@
                     for entry in order[: 2 * (n - 1)]:
                         first_stage(*entry, group)
 
+    direct = [k for k in far_first(far) if min(k, far - k) <= 2]
+
+    def relay(name, slots, low, high):
+        if far > 4:
+            src = (zc + far - 2) % far
+            arrive(name, slots.at[src], src)
+            push(name, low(src), low(src), src, at(df=2))
+            push(name, slots.at[src], slots.at[src], src, at(df=1))
+            src = (zc + 2) % far
+            arrive(name, slots.at[src], src)
+            if high:
+                push(name, high(src), high(src), far, at(df=far - 2))
+            push(name, slots.at[src], slots.at[src], src, at(df=far - 1))
+
+    def settle(name, slots, low, high):
+        for k in range(1, far):
+            src = (zc + k) % far
+            if far <= 4 or k in (1, 3, far - 3, far - 1):
+                arrive(name, slots.at[src], src)
+            elif k == far // 2:
+                arrive(name, low(src), src)
+                if high:
+                    arrive(name, high(src), far)
+
     def gram_far():
         for k in range(n):
             for m in range(zn):
@@ -228,11 +279,9 @@
         for i in range(1, n * zn):
             total = total + gx[i // zn, i % zn]
         gf[zc] = total
-        if far > 4:
-            pl.semaphore_wait(hand.at[1], 2)
-        elif far > 2:
+        if far > 2:
             pl.semaphore_wait(hand.at[0], len(beside))
-        for k in far_first(far):
+        for k in direct:
             push("gf", gf.at[zc], gf.at[zc], zc, at(df=k))
 
     for group in turn:
@@ -277,10 +326,14 @@
         else:
             f1[zc, t3:] = total
 
-    for k in far_first(far):
+    for k in direct:
         push("f1", f1.at[zc], f1.at[zc], zc, at(df=k))
-
-    arrive_all("gf", gf, zc, far)
+    gram_cut = (lambda src: gf.at[src], None)
+    cut = (lambda src: f1.at[src, 0:t3], lambda src: f1.at[src, t3 : 2 * t3])
+    relay("gf", gf, *gram_cut)
+    relay("f1", f1, *cut)
+
+    settle("gf", gf, *gram_cut)
     g = gf[0]
     for k in range(1, far):
         g = g + gf[k]
@@ -306,7 +359,7 @@
     w2 = mid + pltpu.roll(hi, 32, 1)
     w6 = jnp.concatenate([w1, w2], axis=1)[:, : 6 * RANK].astype(BF16)
 
-    arrive_all("f1", f1, zc, far)
+    settle("f1", f1, *cut)
     total = f1[0]
     for k in range(1, far):
         total = total + f1[k]
@@ -407,7 +460,7 @@
     base, total = {}, 0
     for name, count in (
         ("p", n), ("gc", 2), ("gx", n * zn), ("gf", far), ("cr", pieces),
-        ("a1", n * n), ("b1", n * n), ("a2", n * zn), ("b2", n * zn), ("f1", far),
+        ("a1", n * n), ("b1", n * n), ("a2", n * zn), ("b2", n * zn), ("f1", far + 1),
         ("a3", n * zn), ("b3", n * zn), ("a4", n * n), ("b4", n * n),
         ("cg", pieces), ("ch", pieces),
     ):
@@ -452,7 +505,7 @@
             pltpu.SemaphoreType.DMA((4, 3)),
             pltpu.SemaphoreType.DMA((total,)),
             pltpu.SemaphoreType.DMA((total,)),
-            pltpu.SemaphoreType.REGULAR((2,)),
+            pltpu.SemaphoreType.REGULAR((4,)),
         ],
         compiler_params=pltpu.CompilerParams(
             collective_id=0, has_side_effects=True, vmem_limit_bytes=GRANT * 1024

time: 85.1 us -> 82.9 us (0.974)
  Pallas kernels: 84.3 us -> 82.2 us
    pallas_call x1, Pallas kernels: 82.7 us -> 80.6 us  [body(): pl.pallas_call(functools.partial(kernel, (n, zn, far, base, parts)), out_...]
where the time goes in v4:
time: 82.9 us; the launch traced here: 82.8 us
  Pallas kernels  82.2 us (99%)
    pallas_call x1, Pallas kernels, body(): pl.pallas_call(functools.partial(kernel, (n, zn, far, base, parts)), out_...  80.6 us

profile of v4, /device:TPU:1, one launch (start us, length us, event | category | flops | bytes accessed | tf_op | source)
XLA Modules:
  0.0 82.8 jit_solution(1183207679380725178)
XLA Ops:
  0.6 80.6 %powersgd.1 = (f32[8,14336]{1,0:T(8,128)S(1)}, f32[8,14336]{1,0:T(8,128)S(1)}, f32[8,14336]{1,0:T(8,128)S(1)}, f32[8,14336]{1,0:T(8,128)S(1)}, bf16[32,14336]{1,0:T(8,128)(2,1)S(1)}) custom-call(bf16[32,14336]{1,0:T(8,128)(2,1)} %bitcast.5, bf16[32,14336]{1,0:T(8,128)(2,1)} %bitcast.6, f32[32,14336]{1,0:T(8,128)} %bitcast.4), custom_call_target="tpu_custom_call" | custom-call | tf_op jit(solution)/shard_map/powersgd/pallas_call | solution.py:476
  81.2 1.6 %write_out.1 = (f32[32,14336]{1,0:T(8,128)}, bf16[32,14336]{1,0:T(8,128)(2,1)}) custom-call(f32[8,14336]{1,0:T(8,128)S(1)} %get-tuple-element.9.refs_0_, f32[8,14336]{1,0:T(8,128)S(1)} %get-tuple-element.10.refs_1_, f32[8,14336]{1,0:T(8,128)S(1)} %get-tuple-element.11.refs_2_, f32[8,14336]{1,0:T(8,128)S(1)} %get-tuple-element.12.refs_3_, ...), custom_call_target="tpu_custom_call" | custom-call | tf_op jit(solution)/shard_map/write_out/pallas_call | solution.py:515
